TPU v7x, 32 devices: a whole 2x2x4 slice. The times are simulated.
32 devices in a mesh: grp: 2 (over y), dp: 16 (over z, x, core).
Axes of the slice: x: 2, y: 2, z: 4, core: 2. Of those that a mesh axis runs over, the one named last changes fastest.
Arguments:
- params: float32 [1900544], P(('grp', 'dp')), parts along dimension 0, may hold values from -0.3 to 0.3
- momentum: float32 [1900544], P(('grp', 'dp')), parts along dimension 0, may hold values from -6 to 6
- noise_draws: float32 [2, 950272], P('grp', 'dp'), parts along dimension 0, may hold values from -6 to 6
- images: float32 [16384, 448], P(('grp', 'dp')), parts along dimension 0, may hold values from -6 to 6
- labels: int32 [16384], P(('grp', 'dp')), parts along dimension 0, may hold values from 0 to 9
- indices: int32 [2, 4096], P('grp', 'dp'), parts along dimension 0, may hold values from 0 to 511
Outputs:
- params_out: float32 [1900544], P(('grp', 'dp')), parts along dimension 0
- momentum_out: float32 [1900544], P(('grp', 'dp')), parts along dimension 0
- losses: float32 [2], P('grp'), parts along dimension 0
There are 2 independent parts, one for each index of `grp`. A program takes and returns all parts, laid end to end along the dimension named above; each array names one. Nothing has to cross between parts.
All inputs are finite; a program needn't handle non-finite values.
Results may differ from a plain program's by a relative error of at most 0.0003.
Values sent between devices are 32-bit elements; how exact they have to be, the bound alone decides.
A program may use at most 64 MiB of HBM per device.

v0:
```python
import math
import jax
import jax.numpy as jnp
from jax import lax
from jax.sharding import PartitionSpec as P

DIN = 448
H = 2048
OUT = 10
step_size = 0.02
friction = 15.0


def unpack(flat_vec):
    in_end = DIN * H
    w_in = flat_vec[:in_end].reshape(DIN, H)
    b_in = flat_vec[in_end : in_end + H]
    hid_end = in_end + H
    w_out = flat_vec[hid_end : hid_end + H * OUT].reshape(H, OUT)
    b_out = flat_vec[hid_end + H * OUT : hid_end + H * OUT + OUT]
    return (w_in, b_in, w_out, b_out)


def total_nll(flat_vec, chosen_rows, targets):
    w_in, b_in, w_out, b_out = unpack(flat_vec)
    hidden = jnp.tanh(
        jnp.dot(
            chosen_rows, w_in, precision=lax.Precision.HIGHEST, preferred_element_type=jnp.float32
        )
        + b_in
    )
    logits = (
        jnp.dot(hidden, w_out, precision=lax.Precision.HIGHEST, preferred_element_type=jnp.float32)
        + b_out
    )
    log_norm = jnp.log(jnp.sum(jnp.exp(logits), axis=1))
    classes = lax.broadcasted_iota(jnp.int32, logits.shape, 1)
    picked = jnp.sum(jnp.where(targets[:, None] == classes, logits, 0.0), axis=1)
    return jnp.sum(log_norm - picked)


def prior_precision(flat_index):
    in_end = DIN * H
    hid_end = in_end + H
    out_end = hid_end + H * OUT
    return jnp.where(
        flat_index < in_end,
        float(DIN),
        jnp.where(flat_index < hid_end, 1.0, jnp.where(flat_index < out_end, float(H), 1.0)),
    )


def body(params, momentum, noise_draws, images, labels, indices):
    shard_len = params.shape[0]
    shard_start = lax.axis_index("dp") * shard_len
    precision = prior_precision(shard_start + lax.iota(jnp.int32, shard_len))
    scale_data = images.shape[0] / indices.shape[1]
    row_count = lax.axis_size("dp") * indices.shape[1]
    gathered = lax.all_gather(params, "dp", axis=0, tiled=True)
    picked_rows = indices[0]
    chosen_rows = jnp.take(images, picked_rows, axis=0)
    targets = jnp.take(labels, picked_rows, axis=0)
    nll_part, pullback = jax.vjp(
        lambda weights_flat: total_nll(weights_flat, chosen_rows, targets), gathered
    )
    (local_grad,) = pullback(jnp.ones_like(nll_part))
    losses = [lax.psum(nll_part, "dp") / row_count]
    summed = lax.psum(local_grad, "dp")
    own_grad = lax.dynamic_slice_in_dim(summed, shard_start, shard_len)
    total_force = scale_data * own_grad + precision * params
    momentum = (
        (1.0 - step_size * friction) * momentum
        - step_size * total_force
        + math.sqrt(2.0 * friction * step_size) * noise_draws[0]
    )
    params = params + step_size * momentum
    return (params, momentum, jnp.stack(losses))


def solution(mesh):
    placed = (
        P(("grp", "dp")),
        P(("grp", "dp")),
        P("grp", "dp"),
        P(("grp", "dp"), None),
        P(("grp", "dp")),
        P("grp", "dp"),
    )
    return jax.shard_map(
        body,
        mesh=mesh,
        in_specs=placed,
        out_specs=(P(("grp", "dp")), P(("grp", "dp")), P("grp")),
        check_vma=False,
    )
```

profile of v0, /device:TPU:0, one launch (start us, length us, event | category | flops | bytes accessed | tf_op | source)
XLA Modules:
  0.0 212.2 jit_solution(1588823697586954154)
XLA Ops:
  7.2 0.0 copy-start
  7.2 0.0 copy-start.5
  7.2 0.0 all-gather.2.cloned.1.call-start
  7.2 0.7 all-gather.2.cloned.1.call-update
  7.9 0.0 all-reduce.6.cloned.1.call-start
  8.0 1.5 copy.12
  9.5 0.0 copy-done.5
  9.5 0.0 copy-done
  9.5 1.9 gather_fusion
  11.5 1.0 gather_fusion.1
  12.5 48.9 %all-gather.2.cloned.1.call-done = f32[950272]{0:T(1024)} async-done(((f32[59392]{0:T(1024)}), f32[950272]{0:T(1024)}) %all-gather.2.cloned.1.call-update) | async-done | bytes 3801104 | tf_op jit(solution)/shard_map/all_gather | solution.py:59
  61.4 4.1 %slice.31 = f32[917504]{0:T(1024)} slice(f32[950272]{0:T(1024)} %all-gather.2.cloned.1.call-done), slice={[0:917504]} | slice | bytes 7340032 | tf_op jit(solution)/shard_map/jvp()/slice | solution.py:16
  65.5 4.8 %slice.23 = f32[448,2048]{1,0:T(8,128)} reshape(f32[917504]{0:T(1024)} %slice.31) | data formatting | bytes 7340032 | tf_op jit(solution)/shard_map/jvp()/slice | solution.py:16
  70.3 1.0 reshape.81
  71.3 0.0 slice-start.2
  71.3 5.7 %fusion = f32[256,2048]{1,0:T(8,128)S(1)} fusion(f32[448,2048]{1,0:T(8,128)} %slice.23, f32[2048]{0:T(1024)S(1)} %slice-done.1, f32[256,448]{1,0:T(8,128)S(1)} %gather_fusion.1, pred[256]{0:T(512)(128)(4,1)S(1)} %get-tuple-element.8), kind=kOutput, calls=%fused_computation.4 | convolution fusion | flops 2819211264 | bytes 6234368 | tf_op jit(solution)/shard_map/jvp()/dot_general | solution.py:27
  77.1 0.0 slice-done.2
  77.1 1.9 exponential_reduce_fusion
  78.9 0.1 select_reduce_fusion
  79.1 4.5 %fusion.10 = f32[2048,10]{1,0:T(8,128)} fusion(f32[256,2048]{1,0:T(8,128)S(1)} %fusion, f32[256,10]{0,1:T(8,128)S(1)} %get-tuple-element.10, f32[256]{0:T(256)S(1)} %broadcast_divide_fusion, s32[256]{0:T(256)S(1)} %get-tuple-element.7), kind=kOutput, calls=%fused_computation.26 | convolution fusion | flops 62924800 | bytes 2191360 | tf_op jit(solution)/shard_map/transpose(jvp())/dot_general | solution.py:33
  83.6 2.1 fusion.18
  85.7 2.0 reshape.82
  87.7 4.7 %convolution_bitcast_fusion = f32[56,16,8,128]{3,2,1,0:T(8,128)S(1)} fusion(f32[256,2048]{1,0:T(8,128)S(1)} %get-tuple-element.12, f32[256,448]{1,0:T(8,128)} %copy-done.1, pred[256]{0:T(512)(128)(4,1)S(1)} %get-tuple-element.8), kind=kOutput, calls=%fused_computation.6 | convolution fusion | flops 2818686976 | bytes 6226176 | tf_op jit(solution)/shard_map/transpose(jvp())/dot_general | solution.py:27
  92.4 0.8 copy.15
  93.2 2.1 %pad_add_fusion = f32[950272]{0:T(1024)} fusion(f32[917504]{0:T(1024)S(1)} %bitcast.15, f32[2048]{0:T(1024)S(1)} %get-tuple-element.11, f32[20480]{0:T(1024)S(1)} %reshape.82, f32[10]{0:T(128)S(1)} %get-tuple-element.4), kind=kLoop, calls=%fused_computation.2 | loop fusion | flops 2850816 | bytes 7561256 | tf_op jit(solution)/shard_map/transpose(jvp())/add_any | solution.py:16
  95.3 0.0 all-reduce.6.cloned.1.call-update
  95.3 0.9 copy-done.4
  96.2 0.2 broadcast_multiply_fusion
  96.5 0.6 subtract_reduce_fusion
  97.1 32.9 %psum.15 = f32[]{:T(128)} all-reduce(f32[]{:T(128)} %subtract_reduce_fusion), channel_id=1, replica_groups=mesh['grp'=2,'dp'=16] {'dp'}, use_global_device_ids=true, to_apply=%region_6.7 | all-reduce | flops 1 | bytes 8 | tf_op jit(solution)/shard_map/psum | solution.py:67
  130.7 71.6 %all-reduce.6.cloned.1.call-done = f32[950272]{0:T(1024)} async-done(((f32[950272]{0:T(1024)}), f32[950272]{0:T(1024)}) %all-reduce.6.cloned.1.call-update) | async-done | bytes 3801104 | tf_op jit(solution)/shard_map/psum | solution.py:68
  202.3 1.9 multiply_add_fusion
  (15 shorter events, 0.0 us)
Async XLA Ops:
  7.2 2.4 %copy-start = (s32[512]{0:T(512)S(1)}, s32[512]{0:T(512)}, u32[]{:S(2)}) copy-start(s32[512]{0:T(512)} %param.10) | copy-start | bytes 6148
  7.2 2.3 %copy-start.5 = (s32[1,256]{1,0:T(1,128)S(1)}, s32[1,256]{1,0:T(1,128)}, u32[]{:S(2)}) copy-start(s32[1,256]{1,0:T(1,128)} %param.11) | copy-start | bytes 3076
  7.2 54.2 %all-gather.2.cloned.1.call-start = ((), (), s32[]{:S(2)}) async-start(), calls=%async_computation | async-start | bytes 4038656 | tf_op jit(solution)/shard_map/all_gather | solution.py:59
  7.9 194.4 %all-reduce.6.cloned.1.call-start = ((), (), s32[]{:S(2)}) async-start(), calls=%async_computation.1 | async-start | bytes 7602176 | tf_op jit(solution)/shard_map/psum | solution.py:68
  12.5 58.9 %copy-start.1 = (f32[256,448]{1,0:T(8,128)}, f32[256,448]{1,0:T(8,128)S(1)}, u32[]{:S(2)}) copy-start(f32[256,448]{1,0:T(8,128)S(1)} %gather_fusion.1) | copy-start | bytes 1376260
  65.5 4.8 %slice-start = ((f32[950272]{0:T(1024)}), f32[20480]{0:T(1024)S(1)}, s32[]{:S(2)}) async-start(f32[950272]{0:T(1024)} %all-gather.2.cloned.1.call-done), calls=%async_computation.2 | async-start | bytes 163840 | tf_op jit(solution)/shard_map/jvp()/slice | solution.py:19
  65.5 5.8 %slice-start.1 = ((f32[950272]{0:T(1024)}), f32[2048]{0:T(1024)S(1)}, s32[]{:S(2)}) async-start(f32[950272]{0:T(1024)} %all-gather.2.cloned.1.call-done), calls=%async_computation.3 | async-start | bytes 16384 | tf_op jit(solution)/shard_map/jvp()/slice | solution.py:17
  71.3 5.7 %slice-start.2 = ((f32[950272]{0:T(1024)}), f32[10]{0:T(128)S(1)}, s32[]{:S(2)}) async-start(f32[950272]{0:T(1024)} %all-gather.2.cloned.1.call-done), calls=%async_computation.4 | async-start | bytes 1024 | tf_op jit(solution)/shard_map/jvp()/slice | solution.py:20
  95.3 0.9 copy-start.4
  95.3 107.0 %copy-start.2 = (f32[59392]{0:T(1024)S(1)}, f32[59392]{0:T(1024)}, u32[]{:S(2)}) copy-start(f32[59392]{0:T(1024)} %param.6) | copy-start | bytes 712708
  95.3 107.0 %copy-start.3 = (f32[59392]{0:T(1024)S(1)}, f32[59392]{0:T(1024)}, u32[]{:S(2)}) copy-start(f32[59392]{0:T(1024)} %param.7) | copy-start | bytes 712708
Sparse Core Ops, SparseCore 0:
  10.3 51.0 all-gather.1
  95.5 106.8 all-reduce.5
where the time goes:
time: 213 us; the launch traced here: 212 us
  waiting for transfers between devices  121 us (57%)
  blocking collectives  32.9 us (15%)
  matrix products  18.9 us (9%)
  local copies, waits for them, and re-layouts  18.1 us (8%)
  between operations  16 us (8%)
  other arithmetic  5 us (2%)
    psum x1, waiting for transfers between devices, body(): summed = lax.psum(local_grad, 'dp')  71.6 us
    all_gather x1, waiting for transfers between devices, body(): gathered = lax.all_gather(params, 'dp', axis=0, tiled=True)  48.9 us
    psum x1, blocking collectives, body(): losses = [lax.psum(nll_part, 'dp') / row_count]  32.9 us
    dot_general x2, matrix products, total_nll(): jnp.dot(chosen_rows, w_in, precision=lax.Precision.HIGHEST, preferred_ele...  10.4 us
    slice x2, local copies, waits for them, and re-layouts, unpack(): w_in = flat_vec[:in_end].reshape(DIN, H)  8.86 us
    dot_general x3, matrix products, total_nll(): jnp.dot(hidden, w_out, precision=lax.Precision.HIGHEST, preferred_element...  8.5 us
  transfers between devices with their start and end apart: 2, of which 2 were waited for; matrix products, arithmetic and copies ran while one was open for 2% of the time, Pallas kernels for 0%

commit v1 on v0

--- a/solution.py
+++ b/solution.py
@@ -65,7 +65,9 @@
     )
     (local_grad,) = pullback(jnp.ones_like(nll_part))
     losses = [lax.psum(nll_part, "dp") / row_count]
-    summed = lax.psum(local_grad, "dp")
+    summed = local_grad
+    for hop in (1, 2, 4, 8):
+        summed = summed + lax.ppermute(summed, "dp", [(dev, dev ^ hop) for dev in range(16)])
     own_grad = lax.dynamic_slice_in_dim(summed, shard_start, shard_len)
     total_force = scale_data * own_grad + precision * params
     momentum = (

time: 213 us -> 464 us (2.18); the launches traced: 212 us -> 456 us
  blocking collectives: 32.9 us -> 171 us
  waiting for transfers between devices: 121 us -> 221 us
  starting transfers between devices: 0.08 us -> 4.72 us
    ppermute x0 -> x4, waiting for transfers between devices: none -> 172 us  [body(): lax.ppermute(summed, 'dp', [(dev, dev ^ hop) for dev in range(16)])]
    psum x1, blocking collectives: 32.9 us -> 171 us  [body(): losses = [lax.psum(nll_part, 'dp') / row_count]]
    psum x1 -> x0, waiting for transfers between devices: 71.6 us -> none  [body(): summed = lax.psum(local_grad, 'dp')]
    ppermute x0 -> x4, starting transfers between devices: none -> 4.68 us  [body(): lax.ppermute(summed, 'dp', [(dev, dev ^ hop) for dev in range(16)])]
  transfers between devices with their start and end apart: 2 -> 5, of which waited for: 2 -> 4; matrix products, arithmetic and copies ran while one was open for 2% -> 1% of each run, Pallas kernels for 0% -> 0%
where the time goes in v1:
time: 464 us; the launch traced here: 456 us
  waiting for transfers between devices  221 us (48%)
  blocking collectives  171 us (37%)
  local copies, waits for them, and re-layouts  17.8 us (4%)
  matrix products  16.9 us (4%)
  between operations  16 us (3%)
  other arithmetic  9.1 us (2%)
  starting transfers between devices  4.72 us (1%)
    ppermute x4, waiting for transfers between devices, body(): lax.ppermute(summed, 'dp', [(dev, dev ^ hop) for dev in range(16)])  172 us
    psum x1, blocking collectives, body(): losses = [lax.psum(nll_part, 'dp') / row_count]  171 us
    all_gather x1, waiting for transfers between devices, body(): gathered = lax.all_gather(params, 'dp', axis=0, tiled=True)  48.3 us
    dot_general x2, matrix products, total_nll(): jnp.dot(chosen_rows, w_in, precision=lax.Precision.HIGHEST, preferred_ele...  9.28 us
  transfers between devices with their start and end apart: 5, of which 4 were waited for; matrix products, arithmetic and copies ran while one was open for 1% of the time, Pallas kernels for 0%

profile of v1, /device:TPU:0, one launch (start us, length us, event | category | flops | bytes accessed | tf_op | source)
XLA Modules:
  0.0 455.8 jit_solution(3389748035846653038)
XLA Ops:
  7.2 0.7 all-gather.2.cloned.1.call-update
  7.9 1.5 copy.12
  9.4 0.7 compare_select_fusion
  10.1 1.9 gather_fusion
  12.1 1.0 gather_fusion.1
  13.1 48.3 %all-gather.2.cloned.1.call-done = f32[950272]{0:T(1024)} async-done(((f32[59392]{0:T(1024)}), f32[950272]{0:T(1024)}) %all-gather.2.cloned.1.call-update) | async-done | bytes 3801104 | tf_op jit(solution)/shard_map/all_gather | solution.py:59
  61.4 4.1 slice.31
  65.5 4.8 %slice.23 = f32[448,2048]{1,0:T(8,128)} reshape(f32[917504]{0:T(1024)} %slice.31) | data formatting | bytes 7340032 | tf_op jit(solution)/shard_map/jvp()/slice | solution.py:16
  70.3 1.0 reshape.81
  71.3 5.7 %fusion = f32[256,2048]{1,0:T(8,128)S(1)} fusion(f32[448,2048]{1,0:T(8,128)} %slice.23, f32[2048]{0:T(1024)S(1)} %slice-done.1, f32[256,448]{1,0:T(8,128)S(1)} %gather_fusion.1, pred[256]{0:T(512)(128)(4,1)S(1)} %get-tuple-element.8), kind=kOutput, calls=%fused_computation.4 | convolution fusion | flops 2819211264 | bytes 6234368 | tf_op jit(solution)/shard_map/jvp()/dot_general | solution.py:27
  77.1 1.9 exponential_reduce_fusion
  78.9 2.1 fusion.25
  81.1 3.6 fusion.15
  84.7 0.1 select_reduce_fusion
  84.8 3.6 convolution_bitcast_fusion
  88.4 2.6 copy.15
  91.0 0.8 reshape.82
  91.7 2.4 pad_add_fusion
  94.2 0.3 collective-permute-start
  94.5 6.4 %collective-permute-done = f32[950272]{0:T(1024)S(1)} collective-permute-done((f32[950272]{0:T(1024)S(1)}, f32[950272]{0:T(1024)S(1)}, u32[]{:S(2)}, u32[]{:S(2)}) %collective-permute-start) | collective-permute-done | bytes 3801120 | tf_op jit(solution)/shard_map/ppermute | solution.py:70
  100.8 0.4 fusion.23
  101.2 0.6 collective-permute-start.1
  101.9 83.7 %collective-permute-done.1 = f32[950272]{0:T(1024)S(1)} collective-permute-done((f32[950272]{0:T(1024)S(1)}, f32[950272]{0:T(1024)S(1)}, u32[]{:S(2)}, u32[]{:S(2)}) %collective-permute-start.1) | collective-permute-done | bytes 3801120 | tf_op jit(solution)/shard_map/ppermute | solution.py:70
  185.6 0.4 add.97
  186.0 1.8 collective-permute-start.2
  187.8 81.7 %collective-permute-done.2 = f32[950272]{0:T(1024)S(1)} collective-permute-done((f32[950272]{0:T(1024)S(1)}, f32[950272]{0:T(1024)S(1)}, u32[]{:S(2)}, u32[]{:S(2)}) %collective-permute-start.2) | collective-permute-done | bytes 3801120 | tf_op jit(solution)/shard_map/ppermute | solution.py:70
  269.5 2.2 add.98
  271.7 2.0 collective-permute-start.3
  273.7 0.2 broadcast_multiply_fusion
  274.0 0.6 subtract_reduce_fusion
  274.6 170.6 %psum.7 = f32[]{:T(128)} all-reduce(f32[]{:T(128)} %subtract_reduce_fusion), channel_id=1, replica_groups=mesh['grp'=2,'dp'=16] {'dp'}, use_global_device_ids=true, to_apply=%region_5.6 | all-reduce | flops 1 | bytes 8 | tf_op jit(solution)/shard_map/psum | solution.py:67
  445.9 2.0 multiply_add_fusion
  (23 shorter events, 0.1 us)
Async XLA Ops:
  7.2 3.0 copy-start
  7.2 54.2 %all-gather.2.cloned.1.call-start = ((), (), s32[]{:S(2)}) async-start(), calls=%async_computation | async-start | bytes 4038656 | tf_op jit(solution)/shard_map/all_gather | solution.py:59
  7.9 5.2 %copy-start.5 = (s32[1,256]{1,0:T(1,128)S(1)}, s32[1,256]{1,0:T(1,128)}, u32[]{:S(2)}) copy-start(s32[1,256]{1,0:T(1,128)} %param.11) | copy-start | bytes 3076
  65.5 4.8 %slice-start = ((f32[950272]{0:T(1024)}), f32[20480]{0:T(1024)S(1)}, s32[]{:S(2)}) async-start(f32[950272]{0:T(1024)} %all-gather.2.cloned.1.call-done), calls=%async_computation.1 | async-start | bytes 163840 | tf_op jit(solution)/shard_map/jvp()/slice | solution.py:19
  65.5 5.8 %slice-start.1 = ((f32[950272]{0:T(1024)}), f32[2048]{0:T(1024)S(1)}, s32[]{:S(2)}) async-start(f32[950272]{0:T(1024)} %all-gather.2.cloned.1.call-done), calls=%async_computation.2 | async-start | bytes 16384 | tf_op jit(solution)/shard_map/jvp()/slice | solution.py:17
  70.3 6.8 %slice-start.2 = ((f32[950272]{0:T(1024)}), f32[10]{0:T(128)S(1)}, s32[]{:S(2)}) async-start(f32[950272]{0:T(1024)} %all-gather.2.cloned.1.call-done), calls=%async_computation.3 | async-start | bytes 1024 | tf_op jit(solution)/shard_map/jvp()/slice | solution.py:20
  91.7 9.1 %copy-start.1 = (f32[56,16,8,128]{3,1,2,0:T(8,128)S(1)}, f32[56,16,8,128]{3,1,2,0:T(8,128)}, u32[]{:S(2)}) copy-start(f32[56,16,8,128]{3,1,2,0:T(8,128)} %copy.15) | copy-start | bytes 11010052
  94.2 6.7 %collective-permute-start = (f32[950272]{0:T(1024)S(1)}, f32[950272]{0:T(1024)S(1)}, u32[]{:S(2)}, u32[]{:S(2)}) collective-permute-start(f32[950272]{0:T(1024)S(1)} %pad_add_fusion), channel_id=1, source_target_pairs={{0,1},{1,0},{2,3},{3,2},{4,5},{5,4},{6,7},{7,6},{8,9},{9,8},{10,11... | collective-permute-start | bytes 11403272 | tf_op jit(solution)/shard_map/ppermute | solution.py:70
  101.2 84.4 %collective-permute-start.1 = (f32[950272]{0:T(1024)S(1)}, f32[950272]{0:T(1024)S(1)}, u32[]{:S(2)}, u32[]{:S(2)}) collective-permute-start(f32[950272]{0:T(1024)S(1)} %fusion.23), channel_id=1, source_target_pairs={{0,2},{1,3},{2,0},{3,1},{4,6},{5,7},{6,4},{7,5},{8,10},{9,11},{10,... | collective-permute-start | bytes 11403272 | tf_op jit(solution)/shard_map/ppermute | solution.py:70
  186.0 87.7 %copy-start.3 = (f32[1,59392]{1,0:T(1,128)S(1)}, f32[1,59392]{1,0:T(1,128)}, u32[]{:S(2)}) copy-start(f32[1,59392]{1,0:T(1,128)} %param.8) | copy-start | bytes 712708
  186.0 259.9 %copy-start.2 = (f32[59392]{0:T(1024)S(1)}, f32[59392]{0:T(1024)}, u32[]{:S(2)}) copy-start(f32[59392]{0:T(1024)} %param.6) | copy-start | bytes 712708
  186.0 259.9 %copy-start.4 = (f32[59392]{0:T(1024)S(1)}, f32[59392]{0:T(1024)}, u32[]{:S(2)}) copy-start(f32[59392]{0:T(1024)} %param.7) | copy-start | bytes 712708
  186.0 83.5 %collective-permute-start.2 = (f32[950272]{0:T(1024)S(1)}, f32[950272]{0:T(1024)S(1)}, u32[]{:S(2)}, u32[]{:S(2)}) collective-permute-start(f32[950272]{0:T(1024)S(1)} %add.97), channel_id=1, source_target_pairs={{0,4},{1,5},{2,6},{3,7},{4,0},{5,1},{6,2},{7,3},{8,12},{9,13},{10,... | collective-permute-start | bytes 11403272 | tf_op jit(solution)/shard_map/ppermute | solution.py:70
  271.7 174.1 %collective-permute-start.3 = (f32[950272]{0:T(1024)}, f32[950272]{0:T(1024)}, u32[]{:S(2)}, u32[]{:S(2)}) collective-permute-start(f32[950272]{0:T(1024)} %add.98), channel_id=1, source_target_pairs={{0,8},{1,9},{2,10},{3,11},{4,12},{5,13},{6,14},{7,15},{8,0},{9,1},... | collective-permute-start | bytes 11403272 | tf_op jit(solution)/shard_map/ppermute | solution.py:70
Sparse Core Ops, SparseCore 0:
  10.3 51.0 all-gather.1
